TPU v7x, 256 devices: a 8x8x2 block of a 8x8x16 slice. The times are simulated.
256 devices in a mesh: groups: 2 (over z), ep: 16 (over x, core), tp: 8 (over y).
Axes of the slice: x: 8, y: 8, z: 2, core: 2. Of those that a mesh axis runs over, the one named last changes fastest.
The devices are a block of a 8x8x16 slice.
Arguments:
- tokens: bfloat16 [1024, 7168], P(('groups', 'ep')), parts along dimension 0, may hold values from -6 to 6
- w_gate: bfloat16 [16, 7168, 2048], P('ep', None, 'tp'), may hold values from -0.0625 to 0.0625
- w_up: bfloat16 [16, 7168, 2048], P('ep', None, 'tp'), may hold values from -0.0625 to 0.0625
- w_down: bfloat16 [16, 2048, 7168], P('ep', 'tp'), may hold values from -0.1875 to 0.1875
- router_logits: float32 [1024, 8], P(('groups', 'ep')), parts along dimension 0, may hold values from -6 to 6
- expert_ids: int32 [1024, 8], P(('groups', 'ep')), parts along dimension 0, may hold values from 0 to 15, all different within a row; in each aligned block of 32 rows (0 to 31, 32 to 63, ...) at most 24 rows name the same one
- draft_lengths: int32 [128], P(('groups', 'ep')), parts along dimension 0, may hold values from 7 to 8
- accept_mask: int32 [128, 8], P(('groups', 'ep')), parts along dimension 0, may hold values 0 or 1
Outputs:
- mixed: bfloat16 [1024, 7168], P(('groups', 'ep'), 'tp'), parts along dimension 0
- accepted: int32 [2], P('groups'), parts along dimension 0
There are 2 independent parts, one for each index of `groups`. A program takes and returns all parts, laid end to end along the dimension named above; an argument that names none is the same for every part. Nothing has to cross between parts.
Inputs may be any that keep to these rules, and one draw needn't show every extreme that they name: `expert_ids`: each row names 8 different experts. Among the rows of one ep index (aligned blocks of 32 rows) no expert is named by more than 24 rows, and in every draw some expert is named by exactly 24 rows of some block.
All inputs are finite; a program needn't handle non-finite values. No bound on the sum of `accept_mask` on one device may be relied on, other than what follows from the above.
Results may differ from a plain program's by a relative error of at most 0.017.
Values may be sent and summed in bfloat16 or wider, within the bound.
No kernel may reach another device: no remote copies, remote signals or barrier semaphores. Data moves between devices by JAX's collectives and lax.ppermute only.
A program may use at most 128 MiB of HBM per device.

v0:
```python
import jax
import jax.numpy as jnp
from jax import lax
from jax.sharding import PartitionSpec as P

DRAFT = 8
EXPERTS = 16
CAP = 24


def sent_to_all(array, axis):
    copies = jnp.broadcast_to(array, (lax.axis_size(axis), *array.shape))
    return lax.all_to_all(copies, axis, split_axis=0, concat_axis=0, tiled=True)


def of_everyone(array, axis):
    everything = sent_to_all(array, axis)
    return jnp.sum(everything, axis=0)


def per_device(tokens, w_gate, w_up, w_down, router_logits, expert_ids, draft_lengths, accept_mask):
    tok_rows = tokens.shape[0]
    width = tokens.shape[1]
    top = expert_ids.shape[1]
    tp_count = lax.axis_size("tp")
    slice_width = width // tp_count
    live = jnp.arange(DRAFT, dtype=jnp.int32)[None, :] < draft_lengths[:, None]
    live_rows = live.reshape(tok_rows)
    live_tokens = jnp.where(live_rows[:, None], tokens, jnp.zeros((), tokens.dtype))
    sig = jax.nn.sigmoid(router_logits)
    gates = 2.827 * sig / jnp.sum(sig, axis=1, keepdims=True)
    flat_ids = expert_ids.reshape(-1)
    onehot = (flat_ids[:, None] == jnp.arange(EXPERTS, dtype=jnp.int32)[None, :]).astype(jnp.int32)
    rank = jnp.cumsum(onehot, axis=0) - 1
    slot = jnp.sum(rank * onehot, axis=1)
    target = flat_ids * CAP + slot
    source = jnp.arange(tok_rows * top, dtype=jnp.int32) // top
    own_cols = lax.dynamic_slice_in_dim(
        live_tokens, lax.axis_index("tp") * slice_width, slice_width, 1
    )
    sendbuf = jnp.zeros((EXPERTS * CAP, slice_width), tokens.dtype).at[target].set(own_cols[source])
    received = lax.all_to_all(
        sendbuf.reshape(EXPERTS, CAP, slice_width), "ep", split_axis=0, concat_axis=1, tiled=True
    )
    piece = lax.all_gather(received, "tp", axis=2, tiled=True)
    gate_sum = jnp.einsum("emd,edf->emf", piece, w_gate, preferred_element_type=jnp.float32)
    up_sum = jnp.einsum("emd,edf->emf", piece, w_up, preferred_element_type=jnp.float32)
    hidden = (jax.nn.silu(gate_sum) * up_sum).astype(jnp.bfloat16)
    partial_value = jnp.einsum("emf,efd->emd", hidden, w_down, preferred_element_type=jnp.float32)
    expert_out = lax.psum_scatter(
        partial_value.astype(jnp.bfloat16), "tp", scatter_dimension=2, tiled=True
    )
    returned = lax.all_to_all(expert_out, "ep", split_axis=1, concat_axis=0, tiled=True)
    flat_back = returned.reshape(EXPERTS * CAP, returned.shape[2])
    picked = flat_back[target].reshape(tok_rows, top, returned.shape[2])
    mixed = jnp.sum(gates[:, :, None] * picked.astype(jnp.float32), axis=1).astype(jnp.bfloat16)
    passed = accept_mask * live.astype(jnp.int32)
    prefix = jnp.cumprod(passed, axis=1)
    local_count = jnp.sum(prefix)
    total = of_everyone(local_count, "ep")
    accepted = total.reshape(1)
    return (mixed, accepted)


def solution(mesh):
    placed = (
        P(("groups", "ep"), None),
        P("ep", None, "tp"),
        P("ep", None, "tp"),
        P("ep", "tp", None),
        P(("groups", "ep"), None),
        P(("groups", "ep"), None),
        P(("groups", "ep")),
        P(("groups", "ep"), None),
    )
    return jax.shard_map(
        per_device,
        mesh=mesh,
        in_specs=placed,
        out_specs=(P(("groups", "ep"), "tp"), P("groups")),
        check_vma=False,
    )
```

profile of v0, /device:TPU:513, one launch (start us, length us, event | category | flops | bytes accessed | tf_op | source)
XLA Modules:
  0.0 286.3 jit_solution(15594155464627464665)
XLA Ops:
  7.2 0.1 all-gather.2.cloned.1.call-start
  7.2 0.8 copy.36
  8.0 0.1 eq.29
  8.1 0.1 eq.25
  8.2 0.7 broadcast_multiply_fusion
  8.9 0.6 reduce-window.6
  9.5 0.2 slice_reduce_fusion
  9.7 0.1 copy.35
  9.8 0.1 mul.55
  9.9 0.7 iota_compare_fusion.2
  10.6 0.1 lt.48
  10.7 0.1 fusion.23
  10.8 0.9 dynamic-slice_select_fusion
  11.7 3.5 %scatter_custom_fusion = bf16[384,896]{1,0:T(8,128)(2,1)S(1)} fusion(s32[256]{0:T(256)S(1)} %bitcast.67, bf16[32,896]{1,0:T(8,128)(2,1)S(1)} %dynamic-slice_select_fusion, s32[1024]{0:T(1024)S(1)} %pad_clamp_fusion.1, bf16[]{:T(256)} %constant.43.clone.1), kind=kCustom, calls=%fused_computation.19 | custom fusion | bytes 688130 | tf_op jit(solution)/shard_map/scatter | solution.py:41
  15.2 44.7 %all_to_all.27 = bf16[16,24,896]{2,1,0:T(8,128)(2,1)} all-to-all(bf16[16,24,896]{2,1,0:T(8,128)(2,1)S(1)} %bitcast.66), channel_id=1, replica_groups=mesh['groups'=2,'ep'=16,'tp'=8] {'ep'}, dimensions={0} | all-to-all | bytes 1376256 | tf_op jit(solution)/shard_map/all_to_all | solution.py:42
  59.9 0.1 all-gather.2.cloned.1.call-update
  60.0 0.1 reduce-scatter.4.cloned.1.call-start
  60.1 66.0 %all-gather.2.cloned.1.call-done = bf16[1,384,7168]{2,1,0:T(8,128)(2,1)} async-done(((bf16[1,384,896]{2,1,0:T(8,128)(2,1)}), bf16[1,384,7168]{2,1,0:T(8,128)(2,1)}) %all-gather.2.cloned.1.call-update) | async-done | bytes 5505040 | tf_op jit(solution)/shard_map/all_gather | solution.py:45
  126.1 0.0 copy-start.4
  126.1 0.0 copy-start.5
  126.1 5.4 %fusion.3 = f32[384,256]{1,0:T(8,128)S(1)} fusion(bf16[1,384,7168]{2,1,0:T(8,128)(2,1)} %all-gather.2.cloned.1.call-done, bf16[1,7168,256]{2,1,0:T(8,128)(2,1)} %param.9), kind=kOutput, calls=%fused_computation.8 | convolution fusion | flops 1409286144 | bytes 9568256 | tf_op jit(solution)/shard_map/emd,edf->emf/dot_general | solution.py:46
  131.5 0.0 copy-done.4
  131.5 0.9 copy-done.5
  132.4 0.0 copy-start
  132.4 1.6 fusion.13
  134.0 0.4 copy-done
  134.4 4.0 %fusion = bf16[1,384,7168]{2,1,0:T(8,128)(2,1)} fusion(bf16[384,256]{1,0:T(8,128)(2,1)S(1)} %fusion.13, bf16[1,256,7168]{2,1,0:T(8,128)(2,1)S(1)} %copy-done), kind=kOutput, calls=%fused_computation.4 | convolution fusion | flops 1412038656 | bytes 9371648 | tf_op jit(solution)/shard_map/emf,efd->emd/dot_general | solution.py:49
  138.4 24.0 %copy.41 = bf16[1,384,7168]{1,0,2:T(2,128)(2,1)} copy(bf16[1,384,7168]{2,1,0:T(8,128)(2,1)} %fusion) | data formatting | bytes 11010048
  162.4 7.4 %copy.51 = bf16[7168,1,384]{2,0,1:T(8,128)(2,1)} copy(bf16[7168,1,384]{2,1,0:T(2,128)(2,1)} %bitcast.60) | data formatting | bytes 11010048
  169.8 0.0 copy-start.2
  169.8 0.0 copy-start.3
  169.8 0.1 reduce-scatter.4.cloned.1.call-update
  169.9 0.6 copy-done.2
  170.5 0.0 copy-done.3
  170.5 0.1 broadcast_select_fusion
  170.6 0.2 reduce_window.9
  170.8 0.6 reduce_sum.51
  171.4 1.2 broadcast_in_dim.29
  172.6 7.6 %all-to-all-start.2 = ((s32[16,1,1]{2,1,0:T(1,128)}), s32[16,1,1]{2,1,0:T(1,128)S(1)}, u32[]{:S(2)}, u32[]{:S(2)}) async-start(s32[16,1,1]{2,1,0:T(1,128)} %broadcast_in_dim.29), calls=%async_computation.2 | async-start | bytes 16384 | tf_op jit(solution)/shard_map/all_to_all | solution.py:13
  180.2 57.8 %reduce-scatter.4.cloned.1.call-done = bf16[896,384]{1,0:T(8,128)(2,1)} async-done(((bf16[7168,384]{1,0:T(8,128)(2,1)}), bf16[896,384]{1,0:T(8,128)(2,1)}) %reduce-scatter.4.cloned.1.call-update) | async-done | bytes 688144
  238.0 1.8 reshape_bitcast_fusion
  239.8 0.0 copy-start.1
  239.8 2.3 copy.39
  242.1 0.5 broadcast.160
  242.6 4.8 %reduce.3 = bf16[384,896]{1,0:T(8,128)(2,1)S(1)} reduce(bf16[384,1,896]{2,1,0:T(2,128)(2,1)S(1)} %bitcast.63, bf16[]{:T(256)} %broadcast.160), dimensions={1}, to_apply=%bitcast.54.reduce_sub_computation | reduce | bytes 1376258
  247.5 1.0 reshape.202
  248.5 0.0 all-to-all-done.2
  248.5 7.4 %all-to-all-start.1 = ((bf16[16,2,10752]{2,1,0:T(2,128)(2,1)}), bf16[16,2,10752]{2,1,0:T(2,128)(2,1)S(1)}, u32[]{:S(2)}, u32[]{:S(2)}) async-start(bf16[16,2,10752]{2,1,0:T(2,128)(2,1)} %reshape.202), calls=%async_computation.1 | async-start | bytes 1376256 | tf_op jit(solution)/shard_map/all_to_all | solution.py:53
  256.0 0.0 copy-done.1
  256.0 0.1 copy.34
  256.1 0.7 reduce_sum.52
  256.7 19.8 %all-to-all-done.1 = bf16[16,2,10752]{2,1,0:T(2,128)(2,1)S(1)} async-done(((bf16[16,2,10752]{2,1,0:T(2,128)(2,1)}), bf16[16,2,10752]{2,1,0:T(2,128)(2,1)S(1)}, u32[]{:S(2)}, u32[]{:S(2)}) %all-to-all-start.1) | async-done | bytes 688160 | tf_op jit(solution)/shard_map/all_to_all | solution.py:53
  276.6 0.6 reshape.203
  277.2 0.1 copy.52
  277.2 1.2 gather_fusion
  278.4 1.0 fusion.18
  (9 shorter events, 0.1 us)
Async XLA Ops:
  7.2 118.9 %all-gather.2.cloned.1.call-start = ((), (), s32[]{:S(2)}) async-start(), calls=%async_computation.4 | async-start | bytes 6193152 | tf_op jit(solution)/shard_map/all_gather | solution.py:45
  60.0 178.0 %reduce-scatter.4.cloned.1.call-start = ((), (), s32[]{:S(2)}) async-start(), calls=%async_computation.5 | async-start | bytes 6193152
  126.1 5.4 %copy-start.4 = (bf16[1,384,7168]{2,1,0:T(8,128)(2,1)S(1)}, bf16[1,384,7168]{2,1,0:T(8,128)(2,1)}, u32[]{:S(2)}) copy-start(bf16[1,384,7168]{2,1,0:T(8,128)(2,1)} %all-gather.2.cloned.1.call-done) | copy-start | bytes 16515076
  126.1 6.3 %copy-start.5 = (bf16[1,7168,256]{2,1,0:T(8,128)(2,1)S(1)}, bf16[1,7168,256]{2,1,0:T(8,128)(2,1)}, u32[]{:S(2)}) copy-start(bf16[1,7168,256]{2,1,0:T(8,128)(2,1)} %param.10) | copy-start | bytes 11010052
  132.4 2.0 copy-start
  169.8 0.7 copy-start.2
  169.8 0.7 copy-start.3
  172.6 75.9 %all-to-all-start.2 = ((s32[16,1,1]{2,1,0:T(1,128)}), s32[16,1,1]{2,1,0:T(1,128)S(1)}, u32[]{:S(2)}, u32[]{:S(2)}) async-start(s32[16,1,1]{2,1,0:T(1,128)} %broadcast_in_dim.29), calls=%async_computation.2 | async-start | bytes 16384 | tf_op jit(solution)/shard_map/all_to_all | solution.py:13
  239.8 16.2 %copy-start.1 = (f32[32,8]{0,1:T(8,128)S(1)}, f32[32,8]{0,1:T(8,128)}, u32[]{:S(2)}) copy-start(f32[32,8]{0,1:T(8,128)} %param.12) | copy-start | bytes 3076
  248.5 28.1 %all-to-all-start.1 = ((bf16[16,2,10752]{2,1,0:T(2,128)(2,1)}), bf16[16,2,10752]{2,1,0:T(2,128)(2,1)S(1)}, u32[]{:S(2)}, u32[]{:S(2)}) async-start(bf16[16,2,10752]{2,1,0:T(2,128)(2,1)} %reshape.202), calls=%async_computation.1 | async-start | bytes 1376256 | tf_op jit(solution)/shard_map/all_to_all | solution.py:53
Sparse Core Ops, SparseCore 0:
  60.1 65.8 all-gather.1
  170.0 67.9 reduce-scatter.3
where the time goes:
time: 288 us; the launch traced here: 286 us
  waiting for transfers between devices  144 us (50%)
  local copies, waits for them, and re-layouts  47.2 us (16%)
  blocking collectives  44.7 us (16%)
  starting transfers between devices  15.1 us (5%)
  between operations  14.2 us (5%)
  matrix products  10.9 us (4%)
  other arithmetic  10.4 us (4%)
    all_gather x1, waiting for transfers between devices, per_device(): piece = lax.all_gather(received, 'tp', axis=2, tiled=True)  66 us
    unnamed x3, waiting for transfers between devices  57.9 us
    all_to_all x1, blocking collectives, per_device(): lax.all_to_all(sendbuf.reshape(EXPERTS, CAP, slice_width), 'ep', split_ax...  44.7 us
    unnamed x20, local copies, waits for them, and re-layouts  38.2 us
    all_to_all x1, waiting for transfers between devices, per_device(): lax.all_to_all(expert_out, 'ep', split_axis=1, concat_axis=0, tiled=True)  19.8 us
    all_to_all x1, starting transfers between devices, sent_to_all(): return lax.all_to_all(copies, axis, split_axis=0, concat_axis=0, tiled=True)  7.55 us
    all_to_all x1, starting transfers between devices, per_device(): lax.all_to_all(expert_out, 'ep', split_axis=1, concat_axis=0, tiled=True)  7.44 us
  transfers between devices with their start and end apart: 4, of which 3 were waited for; matrix products, arithmetic and copies ran while one was open for 5% of the time, Pallas kernels for 0%

commit v1 on v0

--- a/solution.py
+++ b/solution.py
@@ -6,6 +6,19 @@
 DRAFT = 8
 EXPERTS = 16
 CAP = 24
+
+
+def settle_task_by_axis(w_in):
+    q_next = jnp.concatenate(
+        lax.all_to_all(
+            jnp.stack(tuple((w_in for _ in range(lax.psum(1, axis_name="tp")))), axis=0),
+            "tp",
+            split_axis=0,
+            concat_axis=0,
+        ),
+        2,
+    )
+    return q_next
 
 
 def sent_to_all(array, axis):
@@ -42,7 +55,7 @@
     received = lax.all_to_all(
         sendbuf.reshape(EXPERTS, CAP, slice_width), "ep", split_axis=0, concat_axis=1, tiled=True
     )
-    piece = lax.all_gather(received, "tp", axis=2, tiled=True)
+    piece = settle_task_by_axis(received)
     gate_sum = jnp.einsum("emd,edf->emf", piece, w_gate, preferred_element_type=jnp.float32)
     up_sum = jnp.einsum("emd,edf->emf", piece, w_up, preferred_element_type=jnp.float32)
     hidden = (jax.nn.silu(gate_sum) * up_sum).astype(jnp.bfloat16)

time: 288 us -> 352 us (1.22)
  blocking collectives: 44.7 us -> 172 us
  waiting for transfers between devices: 144 us -> 79 us
  matrix products: 10.9 us -> 14.6 us
  starting transfers between devices: 15.1 us -> 11.4 us
    all_to_all x0 -> x1, blocking collectives: none -> 128 us  [settle_task_by_axis(): lax.all_to_all(jnp.stack(tuple((w_in for _ in range(lax.psum(1, axis_name...]
    all_gather x1 -> x0, waiting for transfers between devices: 66 us -> none  [per_device(): piece = lax.all_gather(received, 'tp', axis=2, tiled=True)]
    dot_general x1, matrix products: 3.96 us -> 13 us  [per_device(): jnp.einsum('emf,efd->emd', hidden, w_down, preferred_element_type=jnp.flo...]
    dot_general x1, matrix products: 5.39 us -> 1.62 us  [per_device(): jnp.einsum('emd,edf->emf', piece, w_gate, preferred_element_type=jnp.floa...]
    all_to_all x1, starting transfers between devices: 7.55 us -> 3.85 us  [sent_to_all(): return lax.all_to_all(copies, axis, split_axis=0, concat_axis=0, tiled=True)]
    unnamed x3 -> x2, waiting for transfers between devices: 57.9 us -> 59.2 us
    unnamed x20 -> x18, local copies, waits for them, and re-layouts: 38.2 us -> 39.2 us
  transfers between devices with their start and end apart: 4 -> 3, of which waited for: 3 -> 2; matrix products, arithmetic and copies ran while one was open for 5% -> 4% of each run, Pallas kernels for 0% -> 0%
where the time goes in v1:
time: 352 us; the launch traced here: 351 us
  blocking collectives  172 us (49%)
  waiting for transfers between devices  79 us (22%)
  local copies, waits for them, and re-layouts  49 us (14%)
  matrix products  14.6 us (4%)
  between operations  14.2 us (4%)
  starting transfers between devices  11.4 us (3%)
  other arithmetic  10.4 us (3%)
    all_to_all x1, blocking collectives, settle_task_by_axis(): lax.all_to_all(jnp.stack(tuple((w_in for _ in range(lax.psum(1, axis_name...  128 us
    unnamed x2, waiting for transfers between devices  59.2 us
    all_to_all x1, blocking collectives, per_device(): lax.all_to_all(sendbuf.reshape(EXPERTS, CAP, slice_width), 'ep', split_ax...  44 us
    unnamed x18, local copies, waits for them, and re-layouts  39.2 us
    all_to_all x1, waiting for transfers between devices, per_device(): lax.all_to_all(expert_out, 'ep', split_axis=1, concat_axis=0, tiled=True)  19.8 us
    dot_general x1, matrix products, per_device(): jnp.einsum('emf,efd->emd', hidden, w_down, preferred_element_type=jnp.flo...  13 us
    all_to_all x1, starting transfers between devices, per_device(): lax.all_to_all(expert_out, 'ep', split_axis=1, concat_axis=0, tiled=True)  7.46 us
  transfers between devices with their start and end apart: 3, of which 2 were waited for; matrix products, arithmetic and copies ran while one was open for 4% of the time, Pallas kernels for 0%

profile of v1, /device:TPU:513, one launch (start us, length us, event | category | flops | bytes accessed | tf_op | source)
XLA Modules:
  0.0 350.7 jit_solution(2645427229953750391)
XLA Ops:
  7.2 0.1 reduce-scatter.4.cloned.1.call-start
  7.2 0.8 copy.48
  8.0 0.1 eq.29
  8.1 0.1 eq.25
  8.2 0.7 broadcast_multiply_fusion
  8.9 0.6 reduce-window.6
  9.5 0.2 slice_reduce_fusion
  9.7 0.1 copy.47
  9.8 0.1 mul.55
  9.9 0.7 iota_compare_fusion.2
  10.6 0.1 lt.48
  10.7 0.1 fusion.17
  10.8 0.9 dynamic-slice_select_fusion
  11.7 3.5 scatter_custom_fusion
  15.2 44.0 %all_to_all.29 = bf16[16,24,896]{2,1,0:T(8,128)(2,1)S(1)} all-to-all(bf16[16,24,896]{2,1,0:T(8,128)(2,1)S(1)} %bitcast.73), channel_id=1, replica_groups=mesh['groups'=2,'ep'=16,'tp'=8] {'ep'}, dimensions={0} | all-to-all | bytes 1376256 | tf_op jit(solution)/shard_map/all_to_all | solution.py:55
  59.2 0.4 copy.51
  59.6 0.5 stack.5
  60.1 0.0 copy-start.1
  60.1 128.1 %all_to_all.30 = bf16[8,1,384,896]{2,3,1,0:T(8,128)(2,1)S(1)} all-to-all(bf16[8,1,384,896]{2,3,1,0:T(8,128)(2,1)S(1)} %stack.5), channel_id=1, replica_groups=mesh['groups'=2,'ep'=16,'tp'=8] {'tp'}, dimensions={0} | all-to-all | bytes 11010048 | tf_op jit(solution)/shard_map/all_to_all | solution.py:13
  188.2 0.0 copy-start
  188.2 2.4 copy-done
  190.6 0.0 copy-done.1
  190.6 1.6 fusion.4
  192.2 13.0 %fusion = bf16[1,384,7168]{2,1,0:T(8,128)(2,1)} fusion(bf16[1,256,7168]{2,1,0:T(8,128)(2,1)} %param.11, bf16[384,7168]{0,1:T(8,128)(2,1)} %bitcast.67, bf16[1,7168,256]{2,1,0:T(8,128)(2,1)} %param.10, f32[384,256]{1,0:T(8,128)S(1)} %fusion.4), kind=kOutput, calls=%fused_computation.4 | convolution fusion | flops 2821914624 | bytes 18743296 | tf_op jit(solution)/shard_map/emf,efd->emd/dot_general | solution.py:62
  205.2 24.0 %copy.55 = bf16[1,384,7168]{1,0,2:T(2,128)(2,1)} copy(bf16[1,384,7168]{2,1,0:T(8,128)(2,1)} %fusion) | data formatting | bytes 11010048
  229.2 7.4 %copy.65 = bf16[7168,1,384]{2,0,1:T(8,128)(2,1)} copy(bf16[7168,1,384]{2,1,0:T(2,128)(2,1)} %bitcast.68) | data formatting | bytes 11010048
  236.6 0.0 copy-start.3
  236.6 0.0 copy-start.4
  236.6 0.1 reduce-scatter.4.cloned.1.call-update
  236.7 0.6 copy-done.3
  237.3 0.0 copy-done.4
  237.3 0.1 broadcast_select_fusion
  237.4 0.2 reduce_window.9
  237.5 0.6 reduce_sum.51
  238.2 1.2 broadcast_in_dim.29
  239.4 3.9 %all-to-all-start.3 = ((s32[16,1,1]{2,1,0:T(1,128)}), s32[16,1,1]{2,1,0:T(1,128)S(1)}, u32[]{:S(2)}, u32[]{:S(2)}) async-start(s32[16,1,1]{2,1,0:T(1,128)} %broadcast_in_dim.29), calls=%async_computation.3 | async-start | bytes 16384 | tf_op jit(solution)/shard_map/all_to_all | solution.py:26
  243.3 59.1 %reduce-scatter.4.cloned.1.call-done = bf16[896,384]{1,0:T(8,128)(2,1)} async-done(((bf16[7168,384]{1,0:T(8,128)(2,1)}), bf16[896,384]{1,0:T(8,128)(2,1)}) %reduce-scatter.4.cloned.1.call-update) | async-done | bytes 688144
  302.4 1.8 reshape_bitcast_fusion
  304.2 0.0 copy-start.2
  304.2 2.3 copy.53
  306.6 0.5 broadcast.162
  307.1 4.8 %reduce.3 = bf16[384,896]{1,0:T(8,128)(2,1)S(1)} reduce(bf16[384,1,896]{2,1,0:T(2,128)(2,1)S(1)} %bitcast.71, bf16[]{:T(256)} %broadcast.162), dimensions={1}, to_apply=%bitcast.50.reduce_sub_computation | reduce | bytes 1376258
  311.9 1.0 reshape.214
  312.9 0.0 all-to-all-done.3
  312.9 7.5 %all-to-all-start.2 = ((bf16[16,2,10752]{2,1,0:T(2,128)(2,1)}), bf16[16,2,10752]{2,1,0:T(2,128)(2,1)S(1)}, u32[]{:S(2)}, u32[]{:S(2)}) async-start(bf16[16,2,10752]{2,1,0:T(2,128)(2,1)} %reshape.214), calls=%async_computation.2 | async-start | bytes 1376256 | tf_op jit(solution)/shard_map/all_to_all | solution.py:66
  320.4 0.0 copy-done.2
  320.4 0.1 copy.46
  320.5 0.7 reduce_sum.52
  321.2 19.8 %all-to-all-done.2 = bf16[16,2,10752]{2,1,0:T(2,128)(2,1)S(1)} async-done(((bf16[16,2,10752]{2,1,0:T(2,128)(2,1)}), bf16[16,2,10752]{2,1,0:T(2,128)(2,1)S(1)}, u32[]{:S(2)}, u32[]{:S(2)}) %all-to-all-start.2) | async-done | bytes 688160 | tf_op jit(solution)/shard_map/all_to_all | solution.py:66
  341.0 0.6 reshape.215
  341.6 0.1 copy.66
  341.7 1.2 gather_fusion
  342.9 1.0 fusion.12
  (9 shorter events, 0.1 us)
Async XLA Ops:
  7.2 295.2 %reduce-scatter.4.cloned.1.call-start = ((), (), s32[]{:S(2)}) async-start(), calls=%async_computation.5 | async-start | bytes 6193152
  60.1 130.5 %copy-start.1 = (bf16[1,7168,256]{2,1,0:T(8,128)(2,1)S(1)}, bf16[1,7168,256]{2,1,0:T(8,128)(2,1)}, u32[]{:S(2)}) copy-start(bf16[1,7168,256]{2,1,0:T(8,128)(2,1)} %param.9) | copy-start | bytes 11010052
  188.2 2.4 copy-start
  236.6 0.7 copy-start.3
  236.6 0.7 copy-start.4
  239.4 73.5 %all-to-all-start.3 = ((s32[16,1,1]{2,1,0:T(1,128)}), s32[16,1,1]{2,1,0:T(1,128)S(1)}, u32[]{:S(2)}, u32[]{:S(2)}) async-start(s32[16,1,1]{2,1,0:T(1,128)} %broadcast_in_dim.29), calls=%async_computation.3 | async-start | bytes 16384 | tf_op jit(solution)/shard_map/all_to_all | solution.py:26
  304.2 16.2 %copy-start.2 = (f32[32,8]{0,1:T(8,128)S(1)}, f32[32,8]{0,1:T(8,128)}, u32[]{:S(2)}) copy-start(f32[32,8]{0,1:T(8,128)} %param.12) | copy-start | bytes 3076
  312.9 28.1 %all-to-all-start.2 = ((bf16[16,2,10752]{2,1,0:T(2,128)(2,1)}), bf16[16,2,10752]{2,1,0:T(2,128)(2,1)S(1)}, u32[]{:S(2)}, u32[]{:S(2)}) async-start(bf16[16,2,10752]{2,1,0:T(2,128)(2,1)} %reshape.214), calls=%async_computation.2 | async-start | bytes 1376256 | tf_op jit(solution)/shard_map/all_to_all | solution.py:66
Sparse Core Ops, SparseCore 0:
  236.8 65.5 reduce-scatter.3
